TPU v7x, 512 devices: a whole 4x8x8 slice. The times are simulated.
512 devices in a mesh: lat: 16 (over x, z_lo, core), lon: 32 (over z_hi, y).
Axes of the slice: x: 4, y: 8, z: 8 (z_hi: 4, z_lo: 2; z = z_hi * 2 + z_lo), core: 2. Of those that a mesh axis runs over, the one named last changes fastest.
Arguments:
- tokens: bfloat16 [4, 224, 128, 1536], P(None, 'lat', 'lon'), may hold values from -400 to 400, as said below
- in_bounds: int32 [17], replicated, may hold values from 0 to 191, as said below
- out_bounds: int32 [17], replicated, may hold values from 0 to 96, as said below
- down_gain: float32 [768], replicated, may hold values from 0.25 to 1.75
- down_bias: float32 [768], replicated, may hold values from -1 to 1
- down_weight: bfloat16 [768, 384], replicated, may hold values from -0.21875 to 0.21875
- up_weight: bfloat16 [384, 768], replicated, may hold values from -0.3125 to 0.3125
- up_gain: float32 [192], replicated, may hold values from 0.25 to 1.75
- up_bias: float32 [192], replicated, may hold values from -1 to 1
- out_weight: bfloat16 [192, 192], replicated, may hold values from -0.4375 to 0.4375
Outputs:
- merged: bfloat16 [4, 128, 64, 3072], P(None, 'lat', 'lon')
- upsampled: bfloat16 [4, 224, 128, 1536], P(None, 'lat', 'lon')
Inputs may be any that keep to these rules, and one draw needn't show every extreme that they name: `tokens`: band b's fine rows stand in its slots from the first one on; slots past the band's count hold values that no output reads. in_bounds[0] = 0, in_bounds[16] = 191; each band has 10 to 14 fine rows, and some band has 14. out_bounds[0] = 0, out_bounds[16] = 96; each band has 4 to 8 merged rows, and some band has 8. For 0 < b < 16, 2 * out_bounds[b] - in_bounds[b] is 1 to 3, and 3 for some b; so merged band b covers fine rows from band b's first on to at most 3 rows past its last (fine row 191 counting as zeros), and band b's fine rows need merged rows from at most 2 rows before merged band b's first up to its last, 2 being reached.
All inputs are finite; a program needn't handle non-finite values.
Results may differ from a plain program's by a relative error of at most 0.0069.
Values may be sent and summed in bfloat16 or wider, within the bound.
A program may use at most 64 MiB of HBM per device.

v0:
```python
import jax
import jax.numpy as jnp
from jax import lax
from jax.sharding import PartitionSpec as P

HALO = 3


def passed_along(value, axis, steps):
    count = lax.axis_size(axis)
    leading, last = (max(0, -steps), min(count, count - steps))
    return lax.ppermute(value, axis, [(source, source + steps) for source in range(leading, last)])


def passed_along_2(value, axis, by):
    size = lax.axis_size(axis)
    return lax.ppermute(value, axis, [(i, (i + by) % size) for i in range(size)])


def layer_norm(values, scale_vec, shift_vec):
    center = jnp.mean(values, axis=-1, keepdims=True)
    spread = jnp.mean(jnp.square(values - center), axis=-1, keepdims=True)
    return (values - center) * lax.rsqrt(spread + 1e-05) * scale_vec + shift_vec


def body(
    tokens,
    in_bounds,
    out_bounds,
    down_gain,
    down_bias,
    down_weight,
    up_weight,
    up_gain,
    up_bias,
    out_weight,
):
    members, slot_rows, columns, packed = tokens.shape
    channels = down_weight.shape[0] // 4
    levels = packed // channels
    merged_slots = slot_rows // 2 + 1
    half_cols = columns // 2
    band_index = lax.axis_index("lat")
    start_in = in_bounds[band_index]
    end_in = in_bounds[band_index + 1]
    start_out = out_bounds[band_index]
    end_out = out_bounds[band_index + 1]
    count_in = end_in - start_in
    count_out = end_out - start_out
    head_rows = tokens[:, :HALO]
    from_below = passed_along(head_rows, "lat", -1)
    stacked = jnp.concatenate([tokens, from_below], axis=1)
    wanted = 2 * start_out + jnp.arange(2 * merged_slots, dtype=jnp.int32)
    position = jnp.where(wanted < end_in, wanted - start_in, wanted - end_in + slot_rows)
    position = jnp.clip(position, 0, slot_rows + HALO - 1)
    extended = jnp.take(stacked, position, axis=1)
    left_edge = passed_along_2(extended[:, :, columns - 1], "lon", 1)
    shifted = jnp.concatenate([left_edge[:, :, None], extended[:, :, : columns - 1]], axis=2)
    pieces = shifted.reshape(members, merged_slots, 2, half_cols, 2, levels, channels)
    pieces = pieces.transpose(0, 1, 3, 5, 4, 2, 6).reshape(-1, 4 * channels)
    normed = layer_norm(pieces.astype(jnp.float32), down_gain, down_bias).astype(jnp.bfloat16)
    merged = jnp.dot(normed, down_weight, preferred_element_type=jnp.float32).astype(jnp.bfloat16)
    merged = merged.reshape(members, merged_slots, half_cols, levels * 2 * channels)
    merged_live = jnp.arange(merged_slots, dtype=jnp.int32) < count_out
    merged = jnp.where(merged_live[None, :, None, None], merged, jnp.zeros((), jnp.bfloat16))
    widened = jnp.dot(
        merged.reshape(-1, 2 * channels), up_weight, preferred_element_type=jnp.float32
    ).astype(jnp.bfloat16)
    widened = widened.reshape(members, merged_slots, half_cols, levels, 2, 2, channels)
    right_edge = passed_along_2(widened[:, :, 0, :, 0], "lon", -1)
    spread_out = widened.transpose(0, 1, 5, 2, 4, 3, 6).reshape(
        members, 2 * merged_slots, columns, packed
    )
    edge_rows = right_edge.transpose(0, 1, 3, 2, 4).reshape(members, 2 * merged_slots, packed)
    expanded = jnp.concatenate([spread_out[:, :, 1:], edge_rows[:, :, None]], axis=2)
    tail_fine = lax.dynamic_slice_in_dim(expanded, 2 * count_out - HALO, HALO, 1)
    fine_up = passed_along(tail_fine, "lat", 1)
    stacked_fine = jnp.concatenate([fine_up, expanded], axis=1)
    wanted_fine = start_in + jnp.arange(slot_rows, dtype=jnp.int32)
    spot = jnp.clip(wanted_fine - 2 * start_out + HALO, 0, 2 * merged_slots + HALO - 1)
    fine_rows = jnp.take(stacked_fine, spot, axis=1)
    fine_levels = fine_rows.reshape(members, slot_rows, columns, levels, channels)
    renormed = layer_norm(fine_levels.astype(jnp.float32), up_gain, up_bias).astype(jnp.bfloat16)
    finished = jnp.dot(
        renormed.reshape(-1, channels), out_weight, preferred_element_type=jnp.float32
    ).astype(jnp.bfloat16)
    finished = finished.reshape(members, slot_rows, columns, packed)
    fine_live = jnp.arange(slot_rows, dtype=jnp.int32) < count_in
    upsampled = jnp.where(fine_live[None, :, None, None], finished, jnp.zeros((), jnp.bfloat16))
    return (merged, upsampled)


def solution(mesh):
    return jax.shard_map(
        body,
        mesh=mesh,
        in_specs=(P(None, "lat", "lon", None), P(), P(), P(), P(), P(), P(), P(), P(), P()),
        out_specs=(P(None, "lat", "lon", None), P(None, "lat", "lon", None)),
        check_vma=False,
    )
```

profile of v0, /device:TPU:1, one launch (start us, length us, event | category | flops | bytes accessed | tf_op | source)
XLA Modules:
  0.0 89.3 jit_solution(2274198000506104797)
XLA Ops:
  0.6 1.0 %slice.15 = bf16[4,3,4,1536]{3,2,1,0:T(4,128)(2,1)S(1)} slice(bf16[4,14,4,1536]{3,2,1,0:T(4,128)(2,1)} %param.10), slice={[0:4], [0:3], [0:4], [0:1536]} | slice | bytes 294912 | tf_op jit(solution)/shard_map/slice | solution.py:50
  1.7 8.7 %collective-permute-start = (bf16[4,3,4,1536]{3,2,1,0:T(4,128)(2,1)S(1)}, bf16[4,3,4,1536]{3,2,1,0:T(4,128)(2,1)S(1)}, u32[]{:S(2)}, u32[]{:S(2)}) collective-permute-start(bf16[4,3,4,1536]{3,2,1,0:T(4,128)(2,1)S(1)} %slice.15), channel_id=1, source_target_pairs={{32,0},{64,32},{96,64},{128,96},{160,128},{192,160},{224,192},{256... | collective-permute-start | bytes 442376 | tf_op jit(solution)/shard_map/ppermute | solution.py:12
  10.4 1.4 %fusion.23 = (s32[1]{0:T(128)}, s32[1]{0:T(128)}, s32[1]{0:T(128)}, s32[1]{0:T(128)}) fusion(s32[17]{0:T(128)} %param.12, s32[]{:T(128)S(6)} %select_n.80, s32[]{:T(128)S(6)} %select_n.81, s32[17]{0:T(128)} %param.11), kind=kLoop, calls=%fused_computation.62 | loop fusion | bytes 40 | tf_op jit(solution)/shard_map/dynamic_slice | solution.py:47
  12.5 1.3 %fusion.18 = s32[16]{0:T(128)S(1)} fusion(s32[]{:T(128)} %bitcast.3, s32[]{:T(128)} %bitcast.2, s32[]{:T(128)} %bitcast.1), kind=kLoop, calls=%fused_computation.55 | loop fusion | flops 160 | bytes 76 | tf_op jit(solution)/shard_map/jit(_take)/jit(_where)/select_n | solution.py:56
  13.8 1.3 %compare_and_fusion.1 = pred[16]{0:T(512)(128)(4,1)S(1)} fusion(s32[]{:T(128)} %bitcast.3, s32[]{:T(128)} %bitcast.2, s32[]{:T(128)} %bitcast.1), kind=kLoop, calls=%fused_computation.51 | loop fusion | flops 208 | bytes 28 | tf_op jit(solution)/shard_map/jit(_take)/and | solution.py:56
  18.4 1.6 %pad_maximum_fusion = bf16[4,17,4,1536]{3,2,1,0:T(4,128)(2,1)S(1)} fusion(bf16[4,3,4,1536]{3,2,1,0:T(4,128)(2,1)S(1)} %collective-permute-done, bf16[4,14,4,1536]{3,2,1,0:T(4,128)(2,1)} %param.10), kind=kLoop, calls=%fused_computation.22 | loop fusion | flops 417792 | bytes 1671168 | tf_op jit(solution)/shard_map/concatenate | solution.py:52
  20.1 1.2 %gather_fusion = bf16[16,4,4,1536]{3,2,1,0:T(4,128)(2,1)S(1)} fusion(bf16[4,17,4,1536]{3,2,1,0:T(4,128)(2,1)S(1)} %pad_maximum_fusion, s32[1024]{0:T(1024)S(1)} %pad_clamp_fusion.1), kind=kCustom, calls=%fused_computation | custom fusion | bytes 1572928 | tf_op jit(solution)/shard_map/jit(_take)/gather | solution.py:56
  22.3 1.9 %collective-permute-start.1 = (bf16[4,16,1536]{2,1,0:T(8,128)(2,1)S(1)}, bf16[4,16,1536]{2,1,0:T(8,128)(2,1)S(1)}, u32[]{:S(2)}, u32[]{:S(2)}) collective-permute-start(bf16[4,16,1536]{2,1,0:T(8,128)(2,1)S(1)} %bitcast.48), channel_id=1, source_target_pairs={{0,1},{1,2},{2,3},{3,4},{4,5},{5,6},{6,7},{7,8},{8,9},{9,10},{10,1... | collective-permute-start | bytes 589832 | tf_op jit(solution)/shard_map/ppermute | solution.py:17
  25.9 13.4 %collective-permute-done.1 = bf16[4,16,1536]{2,1,0:T(8,128)(2,1)S(1)} collective-permute-done((bf16[4,16,1536]{2,1,0:T(8,128)(2,1)S(1)}, bf16[4,16,1536]{2,1,0:T(8,128)(2,1)S(1)}, u32[]{:S(2)}, u32[]{:S(2)}) %collective-permute-start.1) | collective-permute-done | bytes 196640 | tf_op jit(solution)/shard_map/ppermute | solution.py:17
  39.6 1.9 %maximum_convert_fusion = f32[4,16,4,1536]{3,2,0,1:T(4,128)} fusion(bf16[4,16,3,1536]{3,2,0,1:T(4,128)(2,1)S(1)} %bitcast.46, bf16[4,16,1,1536]{3,2,0,1:T(2,128)(2,1)S(1)} %copy.53), kind=kLoop, calls=%fused_computation.23 | loop fusion | flops 1572864 | bytes 2359296 | tf_op jit(solution)/shard_map/convert_element_type | solution.py:61
  41.5 2.2 %reshape.178 = f32[4,8,2,2,2,8,192]{6,5,4,3,0,2,1:T(8,128)S(1)} reshape(f32[4,16,4,1536]{3,2,0,1:T(4,128)} %maximum_convert_fusion) | data formatting | bytes 3145728 | tf_op jit(solution)/shard_map/convert_element_type | solution.py:61
  43.7 2.4 %fusion.22 = f32[4,8,2,8]{3,2,1,0:T(2,128)S(1)} fusion(f32[4,8,2,2,2,8,192]{6,5,4,3,0,2,1:T(8,128)S(1)} %reshape.178), kind=kLoop, calls=%fused_computation.61 | loop fusion | flops 392704 | bytes 1574912 | tf_op jit(solution)/shard_map/reduce_sum | solution.py:21
  46.1 3.3 %copy.76 = f32[4,8,2,2,2,8,192]{6,2,4,5,3,1,0:T(2,128)} copy(f32[4,8,2,2,2,8,192]{6,5,4,3,0,2,1:T(8,128)S(1)} %reshape.178) | data formatting | bytes 3145728 | tf_op jit(solution)/shard_map/convert_element_type | solution.py:61
  49.4 2.6 %multiply_reduce_fusion = f32[4,8,2,8]{3,2,1,0:T(2,128)S(1)} fusion(f32[4,8,2,8]{3,2,1,0:T(2,128)S(1)} %broadcast_multiply_fusion.1, f32[4,8,2,2,2,8,192]{6,5,4,3,0,2,1:T(8,128)S(1)} %reshape.178), kind=kLoop, calls=%fused_computation.6 | loop fusion | flops 1179136 | bytes 1576960 | tf_op jit(solution)/shard_map/reduce_sum | solution.py:22
  52.3 3.2 %reshape.176 = f32[512,768]{1,0:T(8,128)S(1)} reshape(f32[4,8,2,8,2,2,192]{6,5,4,3,2,1,0:T(2,128)} %bitcast.43) | data formatting | bytes 3145728 | tf_op jit(solution)/shard_map/convert_element_type | solution.py:61
  55.5 1.7 %convolution_convert_fusion.2 = bf16[512,384]{1,0:T(8,128)(2,1)S(1)} fusion(bf16[768,384]{1,0:T(8,128)(2,1)} %param.15, f32[512,768]{1,0:T(8,128)S(1)} %reshape.176, f32[768]{0:T(1024)S(1)} %copy-done.2, f32[768]{0:T(1024)S(1)} %copy-done.3, f32[512]{0:T(512)S(1)} %rsqrt.23, f32[512]{0:T(512)S(1)} %div.17), kind=kOutput, calls=%fused_computation.12 | convolution fusion | flops 304152576 | bytes 2566144 | tf_op jit(solution)/shard_map/dot_general | solution.py:62
  59.6 2.1 %collective-permute-start.2 = (bf16[4,8,8,2,192]{4,2,3,1,0:T(8,128)(2,1)}, bf16[4,8,8,2,192]{4,2,3,1,0:T(8,128)(2,1)}, u32[]{:S(2)}, u32[]{:S(2)}) collective-permute-start(bf16[4,8,8,2,192]{4,2,3,1,0:T(8,128)(2,1)} %bitcast.40), channel_id=1, source_target_pairs={{0,31},{1,0},{2,1},{3,2},{4,3},{5,4},{6,5},{7,6},{8,7},{9,8},{10,9... | collective-permute-start | bytes 589832 | tf_op jit(solution)/shard_map/ppermute | solution.py:17
  63.6 6.3 %collective-permute-done.2 = bf16[4,8,8,2,192]{4,2,3,1,0:T(8,128)(2,1)} collective-permute-done((bf16[4,8,8,2,192]{4,2,3,1,0:T(8,128)(2,1)}, bf16[4,8,8,2,192]{4,2,3,1,0:T(8,128)(2,1)}, u32[]{:S(2)}, u32[]{:S(2)}) %collective-permute-start.2) | collective-permute-done | bytes 196640 | tf_op jit(solution)/shard_map/ppermute | solution.py:17
  69.9 1.5 %broadcast_in_dim_reshape.4 = bf16[4,16,1,1536]{3,2,1,0:T(2,128)(2,1)S(1)} reshape(bf16[4,8,2,8,192]{4,3,2,1,0:T(8,128)(2,1)} %bitcast.11) | data formatting | bytes 393216 | tf_op jit(solution)/shard_map/broadcast_in_dim;reshape | solution.py:75
  71.6 4.5 %collective-permute-start.3 = (bf16[4,3,4,1536]{3,2,1,0:T(4,128)(2,1)S(1)}, bf16[4,3,4,1536]{3,2,1,0:T(4,128)(2,1)S(1)}, u32[]{:S(2)}, u32[]{:S(2)}) collective-permute-start(bf16[4,3,4,1536]{3,2,1,0:T(4,128)(2,1)S(1)} %fusion.15), channel_id=1, source_target_pairs={{0,32},{32,64},{64,96},{96,128},{128,160},{160,192},{192,224},{224... | collective-permute-start | bytes 442376 | tf_op jit(solution)/shard_map/ppermute | solution.py:12
  76.1 1.1 %broadcast_select_fusion.1 = bf16[4,8,2,3072]{3,2,1,0:T(2,128)(2,1)} fusion(bf16[4,8,2,3072]{3,2,1,0:T(2,128)(2,1)S(1)} %reshape.172, pred[8]{0:T(512)(128)(4,1)S(1)} %iota_compare_fusion.1), kind=kLoop, calls=%fused_computation.31 | loop fusion | flops 196608 | bytes 786440 | tf_op jit(solution)/shard_map/jit(_where)/select_n | solution.py:65
  79.1 1.1 %gather_fusion.1 = bf16[14,4,4,1536]{3,2,1,0:T(4,128)(2,1)S(1)} fusion(bf16[4,19,4,1536]{3,2,1,0:T(4,128)(2,1)S(1)} %maximum_maximum_fusion, s32[1024]{0:T(1024)S(1)} %pad_clamp_fusion), kind=kCustom, calls=%fused_computation.1 | custom fusion | bytes 1376312 | tf_op jit(solution)/shard_map/jit(_take)/gather | solution.py:81
  84.8 1.9 %convolution_convert_fusion = bf16[1792,192]{0,1:T(8,128)(2,1)S(1)} fusion(bf16[192,192]{1,0:T(8,128)(2,1)S(1)} %copy-done.1, f32[192]{0:T(256)S(1)} %copy-done.4, f32[192]{0:T(256)S(1)} %copy-done.5, f32[1792]{0:T(1024)S(1)} %rsqrt.25, f32[1792]{0:T(1024)S(1)} %div.20, bf16[1792,192]{1,0:T(8,128)(2,1)S(1)} %gather.14, pred[1792]{0:T(1024)(128)(4,1)S(1)} %broadcast_in_dim.76), kind=kOutput, calls=%fused_computation.2 | convolution fusion | flops 134873088 | bytes 1467648 | tf_op jit(solution)/shard_map/dot_general | solution.py:84
  88.1 1.2 %broadcast_select_fusion.2 = bf16[4,14,4,1536]{3,2,1,0:T(4,128)(2,1)} fusion(bf16[4,14,4,1536]{3,2,1,0:T(4,128)(2,1)S(1)} %reshape.175, pred[14]{0:T(512)(128)(4,1)S(1)} %iota_compare_fusion), kind=kLoop, calls=%fused_computation.32 | loop fusion | flops 344064 | bytes 1376270 | tf_op jit(solution)/shard_map/jit(_where)/select_n | solution.py:89
  (59 shorter events, 16.0 us)
Async XLA Ops:
  0.6 56.6 %copy-start = (bf16[384,768]{1,0:T(8,128)(2,1)S(1)}, bf16[384,768]{1,0:T(8,128)(2,1)}, u32[]{:S(2)}) copy-start(bf16[384,768]{1,0:T(8,128)(2,1)} %param.16) | copy-start | bytes 1769476
  1.7 16.7 %collective-permute-start = (bf16[4,3,4,1536]{3,2,1,0:T(4,128)(2,1)S(1)}, bf16[4,3,4,1536]{3,2,1,0:T(4,128)(2,1)S(1)}, u32[]{:S(2)}, u32[]{:S(2)}) collective-permute-start(bf16[4,3,4,1536]{3,2,1,0:T(4,128)(2,1)S(1)} %slice.15), channel_id=1, source_target_pairs={{32,0},{64,32},{96,64},{128,96},{160,128},{192,160},{224,192},{256... | collective-permute-start | bytes 442376 | tf_op jit(solution)/shard_map/ppermute | solution.py:12
  22.3 17.0 %collective-permute-start.1 = (bf16[4,16,1536]{2,1,0:T(8,128)(2,1)S(1)}, bf16[4,16,1536]{2,1,0:T(8,128)(2,1)S(1)}, u32[]{:S(2)}, u32[]{:S(2)}) collective-permute-start(bf16[4,16,1536]{2,1,0:T(8,128)(2,1)S(1)} %bitcast.48), channel_id=1, source_target_pairs={{0,1},{1,2},{2,3},{3,4},{4,5},{5,6},{6,7},{7,8},{8,9},{9,10},{10,1... | collective-permute-start | bytes 589832 | tf_op jit(solution)/shard_map/ppermute | solution.py:17
  52.3 3.2 %copy-start.2 = (f32[768]{0:T(1024)S(1)}, f32[768]{0:T(1024)}, u32[]{:S(2)}) copy-start(f32[768]{0:T(1024)} %param.14) | copy-start | bytes 9220
  52.3 3.2 %copy-start.3 = (f32[768]{0:T(1024)S(1)}, f32[768]{0:T(1024)}, u32[]{:S(2)}) copy-start(f32[768]{0:T(1024)} %param.13) | copy-start | bytes 9220
  59.6 10.3 %collective-permute-start.2 = (bf16[4,8,8,2,192]{4,2,3,1,0:T(8,128)(2,1)}, bf16[4,8,8,2,192]{4,2,3,1,0:T(8,128)(2,1)}, u32[]{:S(2)}, u32[]{:S(2)}) collective-permute-start(bf16[4,8,8,2,192]{4,2,3,1,0:T(8,128)(2,1)} %bitcast.40), channel_id=1, source_target_pairs={{0,31},{1,0},{2,1},{3,2},{4,3},{5,4},{6,5},{7,6},{8,7},{9,8},{10,9... | collective-permute-start | bytes 589832 | tf_op jit(solution)/shard_map/ppermute | solution.py:17
  71.6 6.6 %collective-permute-start.3 = (bf16[4,3,4,1536]{3,2,1,0:T(4,128)(2,1)S(1)}, bf16[4,3,4,1536]{3,2,1,0:T(4,128)(2,1)S(1)}, u32[]{:S(2)}, u32[]{:S(2)}) collective-permute-start(bf16[4,3,4,1536]{3,2,1,0:T(4,128)(2,1)S(1)} %fusion.15), channel_id=1, source_target_pairs={{0,32},{32,64},{64,96},{96,128},{128,160},{160,192},{192,224},{224... | collective-permute-start | bytes 442376 | tf_op jit(solution)/shard_map/ppermute | solution.py:12
  82.2 2.6 %copy-start.1 = (bf16[192,192]{1,0:T(8,128)(2,1)S(1)}, bf16[192,192]{1,0:T(8,128)(2,1)}, u32[]{:S(2)}) copy-start(bf16[192,192]{1,0:T(8,128)(2,1)} %param.19) | copy-start | bytes 221188
  82.2 2.6 %copy-start.4 = (f32[192]{0:T(256)S(1)}, f32[192]{0:T(256)}, u32[]{:S(2)}) copy-start(f32[192]{0:T(256)} %param.18) | copy-start | bytes 2308
  82.2 2.6 %copy-start.5 = (f32[192]{0:T(256)S(1)}, f32[192]{0:T(256)}, u32[]{:S(2)}) copy-start(f32[192]{0:T(256)} %param.17) | copy-start | bytes 2308
where the time goes:
time: 89.8 us; the launch traced here: 89.3 us
  local copies, waits for them, and re-layouts  25 us (28%)
  waiting for transfers between devices  20.7 us (23%)
  other arithmetic  18 us (20%)
  starting transfers between devices  17.3 us (19%)
  between operations  4.26 us (5%)
  matrix products  4.17 us (5%)
    ppermute x2, waiting for transfers between devices, passed_along_2(): lax.ppermute(value, axis, [(i, (i + by) % size) for i in range(size)])  19.7 us
    ppermute x2, starting transfers between devices, passed_along(): lax.ppermute(value, axis, [(source, source + steps) for source in range(l...  13.2 us
    convert_element_type x3, local copies, waits for them, and re-layouts, body(): pieces.astype(jnp.float32)  8.65 us
    ppermute x2, starting transfers between devices, passed_along_2(): lax.ppermute(value, axis, [(i, (i + by) % size) for i in range(size)])  4.05 us
    reduce_sum x2, other arithmetic, layer_norm(): spread = jnp.mean(jnp.square(values - center), axis=-1, keepdims=True)  3.58 us
    reduce_sum x2, other arithmetic, layer_norm(): center = jnp.mean(values, axis=-1, keepdims=True)  2.98 us
    gather x4, local copies, waits for them, and re-layouts, body(): fine_rows = jnp.take(stacked_fine, spot, axis=1)  2.97 us
    convert_element_type x1, other arithmetic, body(): pieces.astype(jnp.float32)  1.92 us
  transfers between devices with their start and end apart: 4, of which 3 were waited for; matrix products, arithmetic and copies ran while one was open for 10% of the time, Pallas kernels for 0%

commit v1 on v0

v1 whole, which is shorter than its diff:
```python
import functools

import jax
import jax.numpy as jnp
from jax import lax
from jax.experimental import pallas as pl
from jax.experimental.pallas import tpu as pltpu
from jax.sharding import PartitionSpec as P

MESH = pl.DeviceIdType.MESH
BF = jnp.bfloat16
F32 = jnp.float32
C = 192
LEV = 8
PAIRS = LEV // 2
E = 4
ROWS = 14
MS = 9
MR = 112
XR = 240


def iota(shape, dim):
    return lax.broadcasted_iota(jnp.int32, shape, dim)


def one_hot(target, width):
    return jnp.where(iota((target.shape[0], width), 1) == target, 1.0, 0.0).astype(BF)


def dot(a, b):
    return jnp.dot(a, b, preferred_element_type=F32)


def pair_sums(v):
    low = iota((v.shape[0], 128), 1) < 64
    mid = v[:, 128:256]
    even = v[:, 0:128] + jnp.where(low, mid, 0.0)
    odd = v[:, 256:384] + jnp.where(low, 0.0, mid)
    return jnp.sum(even, axis=1, keepdims=True), jnp.sum(odd, axis=1, keepdims=True)


def pair_lanes(even, odd, rows):
    low = iota((rows, 128), 1) < 64
    e = jnp.broadcast_to(even, (rows, 128))
    o = jnp.broadcast_to(odd, (rows, 128))
    return jnp.concatenate([e, jnp.where(low, e, o), o], axis=1)


def kernel(
    n_lat,
    n_lon,
    tok,
    inb,
    outb,
    dgain,
    dbias,
    dw,
    uw,
    ugain,
    ubias,
    ow,
    merged,
    ups,
    xs,
    hb,
    ha,
    sb,
    sa,
    g,
    ne,
    no,
    we,
    wo,
    ua,
    ub,
    uc,
    bd,
    co,
    yy,
    ee,
    rn,
    send_sem,
    recv_sem,
):
    lat = lax.axis_index("lat")
    lon = lax.axis_index("lon")
    north = lax.rem(lat + n_lat - 1, n_lat)
    south = lax.rem(lat + 1, n_lat)
    west = lax.rem(lon + n_lon - 1, n_lon)
    east = lax.rem(lon + 1, n_lon)
    around = [
        (north, west),
        (north, lon),
        (north, east),
        (lat, west),
        (lat, east),
        (south, west),
        (south, lon),
        (south, east),
    ]
    barrier = pltpu.get_barrier_semaphore()
    for where in around:
        pl.semaphore_signal(barrier, inc=1, device_id=where, device_id_type=MESH)

    start_in = inb[lat]
    count_in = inb[lat + 1] - start_in
    end_all = inb[n_lat]
    start_out = outb[lat]
    count_out = outb[lat + 1] - start_out
    start_m = start_in >> 1
    par = start_in & 1
    skip_m = start_out - start_m

    zero8 = jnp.zeros((8, LEV * C), BF)
    for x in (3, 0, 1, 2):
        col = x + 1
        j, c = col // 2, col % 2
        xs[c, j * 64 + 56 : j * 64 + 64, :] = zero8
        xs[c, j * 64 : j * 64 + 56, :] = tok[:, :, x, :].reshape(56, LEV * C)
    for x in range(4):
        sb[x] = tok[:, 0:3, x, :].reshape(12, LEV * C)
    for e in range(E):
        last = tok[e, jnp.clip(count_in - 1, 0, ROWS - 1)]
        for x in range(4):
            sa[x, e : e + 1, :] = last[x : x + 1, :]

    pl.semaphore_wait(barrier, 8)

    def send(k, src, dst, where):
        return pltpu.make_async_remote_copy(
            src_ref=src,
            dst_ref=dst,
            send_sem=send_sem.at[k],
            recv_sem=recv_sem.at[k],
            device_id=where,
            device_id_type=MESH,
        )

    copies = [
        send(0, xs.at[0, 128:192], xs.at[0, 0:64], (lat, east)),
        send(1, xs.at[1, 0:64], xs.at[1, 128:192], (lat, west)),
        send(2, sb, hb.at[1:5], (north, lon)),
        send(3, sa, ha.at[1:5], (south, lon)),
        send(4, sb.at[3], hb.at[0], (north, east)),
        send(5, sb.at[0], hb.at[5], (north, west)),
        send(6, sa.at[3], ha.at[0], (south, east)),
        send(7, sa.at[0], ha.at[5], (south, west)),
    ]
    for copy in copies:
        copy.start()

    for q in range(4):
        block = dw[q * C : (q + 1) * C, :]
        zero = jnp.zeros((64, 2 * C), BF)
        we[q * 256 : q * 256 + C, :] = block
        we[q * 256 + C : (q + 1) * 256, :] = zero
        wo[q * 256 : q * 256 + 64, :] = zero
        wo[q * 256 + 64 : (q + 1) * 256, :] = block
    zero64 = jnp.zeros((2 * C, 64), BF)
    for c in range(2):
        for a in range(2):
            q = c * 2 + a
            block = uw[:, q * C : (q + 1) * C]
            at = a * 128
            ua[c, :, at : at + 128] = block[:, 0:128]
            ub[c, 0 : 2 * C, at : at + 128] = jnp.concatenate([block[:, 128:192], zero64], axis=1)
            ub[c, 2 * C : 4 * C, at : at + 128] = jnp.concatenate([zero64, block[:, 0:64]], axis=1)
            uc[c, :, at : at + 128] = block[:, 64:192]
    zero_c = jnp.zeros((C, C), BF)
    small = ow[...]
    bd[0:C, :] = jnp.concatenate([small, zero_c], axis=1)
    bd[C : 2 * C, :] = jnp.concatenate([zero_c, small], axis=1)

    row = iota((MR, 1), 0)
    j = (row >= 36).astype(jnp.int32) + (row >= 72).astype(jnp.int32)
    rest = row - 36 * j
    m = rest >> 2
    e = rest & 3
    picks = []
    for a in range(2):
        off = 2 * m + a - par
        own = j * 64 + e * 14 + off
        below = 192 + j * 16 + e * 3 + (off - count_in)
        above = 192 + j * 16 + 12 + e
        is_own = (off >= 0) & (off < count_in)
        is_below = (off >= count_in) & (off < count_in + 3) & (start_in + off < end_all)
        target = jnp.where(is_own, own, jnp.where(is_below, below, jnp.where(off < 0, above, -1)))
        target = jnp.where(m < MS, target, -1)
        picks.append(one_hot(target, XR))

    for copy in copies:
        copy.wait()

    for col in range(6):
        j, c = col // 2, col % 2
        xs[c, 192 + j * 16 : 208 + j * 16, :] = jnp.concatenate([hb[col], ha[col]], axis=0)

    for c in range(2):
        for a in range(2):
            g[c * 2 + a] = dot(picks[a], xs[c]).astype(BF)

    gains = []
    for q in range(4):
        one_g = dgain[0:1, q * C : (q + 1) * C]
        one_b = dbias[0:1, q * C : (q + 1) * C]
        gains.append((jnp.concatenate([one_g, one_g], axis=1), jnp.concatenate([one_b, one_b], axis=1)))

    def norm_down(step, carry):
        rows = pl.ds(pl.multiple_of(step * 16, 16), 16)
        for lp in range(PAIRS):
            vals = [g[q, rows, lp * 384 : (lp + 1) * 384].astype(F32) for q in range(4)]
            even, odd = pair_sums((vals[0] + vals[1]) + (vals[2] + vals[3]))
            mean = pair_lanes(even * (1.0 / 768), odd * (1.0 / 768), 16)
            vals = [v - mean for v in vals]
            even, odd = pair_sums(
                (vals[0] * vals[0] + vals[1] * vals[1]) + (vals[2] * vals[2] + vals[3] * vals[3])
            )
            rstd = pair_lanes(
                lax.rsqrt(even * (1.0 / 768) + 1e-05), lax.rsqrt(odd * (1.0 / 768) + 1e-05), 16
            )
            at = pl.ds(pl.multiple_of(lp * MR + step * 16, 16), 16)
            for q in range(4):
                out = (vals[q] * rstd * gains[q][0] + gains[q][1]).astype(BF)
                ne[at, q * 256 : (q + 1) * 256] = out[:, 0:256]
                no[at, q * 256 : (q + 1) * 256] = out[:, 128:384]
        return carry

    lax.fori_loop(0, MR // 16, norm_down, 0)
    co[:, 0:384] = dot(ne[...], we[...]).astype(BF)
    co[:, 384:768] = dot(no[...], wo[...]).astype(BF)

    row = iota((64, 1), 0)
    e = row >> 4
    k = (row >> 1) & 7
    target = (row & 1) * 36 + (k + skip_m) * 4 + e
    pick = one_hot(jnp.where(k < count_out, target, -1), MR)
    for lp in range(PAIRS):
        part = dot(pick, co[lp * MR : (lp + 1) * MR, :]).astype(BF)
        merged[:, :, :, lp * 768 : (lp + 1) * 768] = part.reshape(E, 8, 2, 768)

    for c in range(2):
        for t in range(3):
            if t == 0:
                part = dot(co[:, 0:384], ua[c])
            elif t == 1:
                part = dot(co[...], ub[c])
            else:
                part = dot(co[:, 384:768], uc[c])
            part = part.astype(BF)
            for a in range(2):
                for lp in range(PAIRS):
                    yy[(c * 2 + a) * MR : (c * 2 + a + 1) * MR, lp * 384 + t * 128 : lp * 384 + (t + 1) * 128] = part[
                        lp * MR : (lp + 1) * MR, a * 128 : (a + 1) * 128
                    ]
    row = iota((224, 1), 0)
    e = (row >= 56).astype(jnp.int32) + (row >= 112).astype(jnp.int32) + (row >= 168).astype(jnp.int32)
    k = (row - 56 * e) >> 2
    x1 = (row & 3) + 1
    o = k + par
    target = ((x1 & 1) * 2 + (o & 1)) * MR + (x1 >> 1) * 36 + (o >> 1) * 4 + e
    live = k < count_in
    pick = one_hot(jnp.where(live, target, -1), 4 * MR)
    ee[...] = dot(pick, yy[...]).astype(BF)

    gain2 = jnp.concatenate([ugain[...], ugain[...]], axis=1)
    bias2 = jnp.concatenate([ubias[...], ubias[...]], axis=1)

    def norm_up(step, carry):
        rows = pl.ds(pl.multiple_of(step * 16, 16), 16)
        for lp in range(PAIRS):
            v = ee[rows, lp * 384 : (lp + 1) * 384].astype(F32)
            even, odd = pair_sums(v)
            v = v - pair_lanes(even * (1.0 / C), odd * (1.0 / C), 16)
            even, odd = pair_sums(v * v)
            rstd = pair_lanes(
                lax.rsqrt(even * (1.0 / C) + 1e-05), lax.rsqrt(odd * (1.0 / C) + 1e-05), 16
            )
            at = pl.ds(pl.multiple_of(lp * 224 + step * 16, 16), 16)
            rn[at, :] = (v * rstd * gain2 + bias2).astype(BF)
        return carry

    lax.fori_loop(0, 14, norm_up, 0)
    for lp in range(PAIRS):
        part = rn[lp * 224 : (lp + 1) * 224, :]
        left = dot(part, bd[:, 0:256])
        right = dot(part[:, 128:384], bd[128:384, 256:384])
        whole = jnp.where(live, jnp.concatenate([left, right], axis=1), 0.0).astype(BF)
        ups[:, :, :, lp * 384 : (lp + 1) * 384] = whole.reshape(E, ROWS, 4, 384)


def solution(mesh):
    n_lat, n_lon = mesh.shape["lat"], mesh.shape["lon"]
    vmem = pl.BlockSpec(memory_space=pltpu.VMEM)
    smem = pl.BlockSpec(memory_space=pltpu.SMEM)

    def body(tok, inb, outb, dgain, dbias, dw, uw, ugain, ubias, ow):
        wide = LEV * C
        return pl.pallas_call(
            functools.partial(kernel, n_lat, n_lon),
            out_shape=(
                jax.ShapeDtypeStruct((E, 8, 2, 2 * wide), BF),
                jax.ShapeDtypeStruct((E, ROWS, 4, wide), BF),
            ),
            in_specs=[vmem, smem, smem] + [vmem] * 7,
            out_specs=(vmem, vmem),
            scratch_shapes=[
                pltpu.VMEM((2, XR, wide), BF),
                pltpu.VMEM((6, 12, wide), BF),
                pltpu.VMEM((6, 4, wide), BF),
                pltpu.VMEM((4, 12, wide), BF),
                pltpu.VMEM((4, 4, wide), BF),
                pltpu.VMEM((4, MR, wide), BF),
                pltpu.VMEM((4 * MR, 1024), BF),
                pltpu.VMEM((4 * MR, 1024), BF),
                pltpu.VMEM((1024, 384), BF),
                pltpu.VMEM((1024, 384), BF),
                pltpu.VMEM((2, 384, 256), BF),
                pltpu.VMEM((2, 768, 256), BF),
                pltpu.VMEM((2, 384, 256), BF),
                pltpu.VMEM((384, 384), BF),
                pltpu.VMEM((4 * MR, 768), BF),
                pltpu.VMEM((4 * MR, wide), BF),
                pltpu.VMEM((224, wide), BF),
                pltpu.VMEM((4 * 224, 384), BF),
                pltpu.SemaphoreType.DMA((8,)),
                pltpu.SemaphoreType.DMA((8,)),
            ],
            compiler_params=pltpu.CompilerParams(
                collective_id=0, has_side_effects=True, vmem_limit_bytes=60000000
            ),
        )(
            tok,
            inb,
            outb,
            dgain.reshape(1, -1),
            dbias.reshape(1, -1),
            dw,
            uw,
            ugain.reshape(1, -1),
            ubias.reshape(1, -1),
            ow,
        )

    return jax.shard_map(
        body,
        mesh=mesh,
        in_specs=(P(None, "lat", "lon", None), P(), P(), P(), P(), P(), P(), P(), P(), P()),
        out_specs=(P(None, "lat", "lon", None), P(None, "lat", "lon", None)),
        check_vma=False,
    )
```

time: 89.8 us -> 44 us (0.49)
  Pallas kernels: 0 us -> 38.3 us
  waiting for transfers between devices: 20.7 us -> 0 us
  local copies, waits for them, and re-layouts: 25 us -> 4.79 us
  other arithmetic: 18 us -> 0 us
  starting transfers between devices: 17.3 us -> 0 us
  matrix products: 4.17 us -> 0 us
  between operations: 4.26 us -> 0.66 us
    pallas_call x0 -> x1, Pallas kernels: none -> 38.3 us  [body(): pl.pallas_call(functools.partial(kernel, n_lat, n_lon), out_shape=(jax.Sh...]
    ppermute x4 -> x0, waiting for transfers between devices: 20.7 us -> none  [the longest x2 19.7 us: passed_along_2(): lax.ppermute(value, axis, [(i, (i + by) % size) for i in range(size)])]
    ppermute x4 -> x0, starting transfers between devices: 17.3 us -> none  [the longest x2 13.2 us: passed_along(): lax.ppermute(value, axis, [(source, source + steps) for source in range(l...]
    convert_element_type x4 -> x0, local copies, waits for them, and re-layouts: 9.17 us -> none  [the longest x3 8.65 us: body(): pieces.astype(jnp.float32)]
    reduce_sum x4 -> x0, other arithmetic: 6.56 us -> none  [the longest x2 3.58 us: layer_norm(): spread = jnp.mean(jnp.square(values - center), axis=-1, keepdims=True)]
    select_n x5 -> x0, other arithmetic: 4.73 us -> none  [the longest x2 1.69 us: body(): extended = jnp.take(stacked, position, axis=1)]
    gather x5 -> x0, local copies, waits for them, and re-layouts: 4.19 us -> none  [the longest x4 2.97 us: body(): fine_rows = jnp.take(stacked_fine, spot, axis=1)]
    dot_general x3 -> x0, matrix products: 4.17 us -> none  [the longest x1 1.88 us: body(): jnp.dot(renormed.reshape(-1, channels), out_weight, preferred_element_typ...]
  transfers between devices with their start and end apart: 4 -> 0, of which waited for: 3 -> 0; matrix products, arithmetic and copies ran while one was open for 10% -> 0% of each run, Pallas kernels for 0% -> 0%
where the time goes in v1:
time: 44 us; the launch traced here: 43.8 us
  Pallas kernels  38.3 us (87%)
  local copies, waits for them, and re-layouts  4.79 us (11%)
  between operations  0.66 us (2%)
    pallas_call x1, Pallas kernels, body(): pl.pallas_call(functools.partial(kernel, n_lat, n_lon), out_shape=(jax.Sh...  38.3 us
    unnamed x6, local copies, waits for them, and re-layouts  2.93 us
    reshape x1, local copies, waits for them, and re-layouts, body(): dgain.reshape(1, -1)  1.27 us

profile of v1, /device:TPU:1, one launch (start us, length us, event | category | flops | bytes accessed | tf_op | source)
XLA Modules:
  0.0 43.8 jit_solution(12409362539672958870)
XLA Ops:
  0.6 0.0 copy-start.1
  0.6 1.3 %reshape.16.dgain = f32[1,768]{1,0:T(1,128)} reshape(f32[768]{0:T(1024)} %param.13) | data formatting | bytes 6144 | tf_op jit(solution)/shard_map/reshape | solution.py:336
  1.9 0.0 copy-done.1
  1.9 0.6 %reshape.17.dbias = f32[1,768]{1,0:T(1,128)} reshape(f32[768]{0:T(1024)S(1)} %copy-done.1) | data formatting | bytes 6144 | tf_op jit(solution)/shard_map/reshape | solution.py:337
  2.5 38.3 %shard_map.113 = (bf16[4,8,2,3072]{3,2,1,0:T(2,128)(2,1)}, bf16[4,14,4,1536]{3,2,1,0:T(4,128)(2,1)}) custom-call(bf16[4,14,4,1536]{3,2,1,0:T(4,128)(2,1)} %tok.1, s32[17]{0:T(128)} %inb.1, s32[17]{0:T(128)} %outb.1, f32[1,768]{1,0:T(1,128)} %reshape.16.dgain, f32[1,768]{1,0:T(1,128)} %reshape.17.dbias, bf16[768,384]{1,0:T(8,128)(2,1)} %dw.1, ...), custom_call_target="tpu_custom_call" | custom-call | tf_op jit(solution)/shard_map/pallas_call | solution.py:299
  40.8 0.0 copy-start
  40.8 2.1 %copy.14 = bf16[4,8,2,3072]{3,2,1,0:T(2,128)(2,1)} copy(bf16[4,8,2,3072]{3,2,1,0:T(2,128)(2,1)} %get-tuple-element.4) | data formatting | bytes 786432
  42.9 0.0 copy-done
  42.9 0.8 %copy.15 = bf16[4,14,4,1536]{3,2,1,0:T(4,128)(2,1)} copy(bf16[4,14,4,1536]{3,2,1,0:T(4,128)(2,1)S(1)} %copy-done) | data formatting | bytes 1376256
Async XLA Ops:
  0.6 1.3 %copy-start.1 = (f32[768]{0:T(1024)S(1)}, f32[768]{0:T(1024)}, u32[]{:S(2)}) copy-start(f32[768]{0:T(1024)} %param.14) | copy-start | bytes 9220
  40.8 2.1 %copy-start = (bf16[4,14,4,1536]{3,2,1,0:T(4,128)(2,1)S(1)}, bf16[4,14,4,1536]{3,2,1,0:T(4,128)(2,1)}, u32[]{:S(2)}) copy-start(bf16[4,14,4,1536]{3,2,1,0:T(4,128)(2,1)} %get-tuple-element.5) | copy-start | bytes 2064388

commit v2 on v1

v2 whole, which is shorter than its diff:
```python
import functools

import jax
import jax.numpy as jnp
from jax import lax
from jax.experimental import pallas as pl
from jax.experimental.pallas import tpu as pltpu
from jax.sharding import PartitionSpec as P

MESH = pl.DeviceIdType.MESH
BF = jnp.bfloat16
F32 = jnp.float32
C = 192
LEV = 8
PAIRS = LEV // 2
E = 4
ROWS = 14
MS = 9
AR = 80
SEND = 56
BR = 48


def iota(shape, dim):
    return lax.broadcasted_iota(jnp.int32, shape, dim)


def one_hot(target, width):
    return jnp.where(iota((target.shape[0], width), 1) == target, 1.0, 0.0).astype(BF)


def dot(a, b):
    return jnp.dot(a, b, preferred_element_type=F32)


def pair_sums(v):
    low = iota((v.shape[0], 128), 1) < 64
    mid = v[:, 128:256]
    even = v[:, 0:128] + jnp.where(low, mid, 0.0)
    odd = v[:, 256:384] + jnp.where(low, 0.0, mid)
    return jnp.sum(even, axis=1, keepdims=True), jnp.sum(odd, axis=1, keepdims=True)


def pair_lanes(even, odd, rows):
    low = iota((rows, 128), 1) < 64
    e = jnp.broadcast_to(even, (rows, 128))
    o = jnp.broadcast_to(odd, (rows, 128))
    return jnp.concatenate([e, jnp.where(low, e, o), o], axis=1)


def norm_rows(src, rows, ne, no, stack, gains, count):
    def step(i, carry):
        at = pl.ds(pl.multiple_of(i * 16, 16), 16)
        for lp in range(PAIRS):
            vals = [src[q, at, lp * 384 : (lp + 1) * 384].astype(F32) for q in range(4)]
            even, odd = pair_sums((vals[0] + vals[1]) + (vals[2] + vals[3]))
            mean = pair_lanes(even * (1.0 / 768), odd * (1.0 / 768), 16)
            vals = [v - mean for v in vals]
            even, odd = pair_sums(
                (vals[0] * vals[0] + vals[1] * vals[1]) + (vals[2] * vals[2] + vals[3] * vals[3])
            )
            rstd = pair_lanes(
                lax.rsqrt(even * (1.0 / 768) + 1e-05), lax.rsqrt(odd * (1.0 / 768) + 1e-05), 16
            )
            to = pl.ds(pl.multiple_of(lp * stack + i * 16, 16), 16)
            for q in range(4):
                out = (vals[q] * rstd * gains[q][0] + gains[q][1]).astype(BF)
                ne[to, q * 256 : (q + 1) * 256] = out[:, 0:256]
                no[to, q * 256 : (q + 1) * 256] = out[:, 128:384]
        return carry

    lax.fori_loop(0, count, step, 0)


def norm_fine(src, rn, stack, gain2, bias2, count):
    def step(i, carry):
        at = pl.ds(pl.multiple_of(i * 16, 16), 16)
        for lp in range(PAIRS):
            v = src[at, lp * 384 : (lp + 1) * 384].astype(F32)
            even, odd = pair_sums(v)
            v = v - pair_lanes(even * (1.0 / C), odd * (1.0 / C), 16)
            even, odd = pair_sums(v * v)
            rstd = pair_lanes(
                lax.rsqrt(even * (1.0 / C) + 1e-05), lax.rsqrt(odd * (1.0 / C) + 1e-05), 16
            )
            to = pl.ds(pl.multiple_of(lp * stack + i * 16, 16), 16)
            rn[to, :] = (v * rstd * gain2 + bias2).astype(BF)
        return carry

    lax.fori_loop(0, count, step, 0)


def expand(left, both, right, ua, ub, uc, c, yy, base, rows):
    for t in range(3):
        if t == 0:
            part = dot(left, ua[c])
        elif t == 1:
            part = dot(both, ub[c])
        else:
            part = dot(right, uc[c])
        part = part.astype(BF)
        for a in range(2):
            for lp in range(PAIRS):
                yy[base + a * rows : base + (a + 1) * rows, lp * 384 + t * 128 : lp * 384 + (t + 1) * 128] = part[
                    lp * rows : (lp + 1) * rows, a * 128 : (a + 1) * 128
                ]


def project(rn, stack, bd, fs, base, rows):
    left = dot(rn[...], bd[:, 0:256]).astype(BF)
    right = dot(rn[:, 128:384], bd[128:384, 256:384]).astype(BF)
    for lp in range(PAIRS):
        fs[base : base + rows, lp * 384 : lp * 384 + 256] = left[lp * stack : lp * stack + rows, :]
        fs[base : base + rows, lp * 384 + 256 : (lp + 1) * 384] = right[lp * stack : lp * stack + rows, :]


def kernel(
    n_lat,
    n_lon,
    tok_hbm,
    inb_hbm,
    outb_hbm,
    dgain_hbm,
    dbias_hbm,
    dw_hbm,
    uw_hbm,
    ugain_hbm,
    ubias_hbm,
    ow_hbm,
    merged,
    ups,
    inb,
    outb,
    dgain,
    dbias,
    ugain,
    ubias,
    tok,
    dw,
    uw,
    ow,
    xa,
    xb,
    sc,
    ew,
    ee,
    ls,
    ln,
    cws,
    cwn,
    ces,
    cen,
    ga,
    gb,
    nea,
    noa,
    neb,
    nob,
    we,
    wo,
    ua,
    ub,
    uc,
    bd,
    coa,
    cob,
    ya,
    yb,
    ea,
    eb,
    rna,
    rnb,
    fs,
    load_sem,
    send_sem,
    recv_sem,
):
    lat = lax.axis_index("lat")
    lon = lax.axis_index("lon")
    north = (lax.rem(lat + n_lat - 1, n_lat), lon)
    south = (lax.rem(lat + 1, n_lat), lon)
    west = (lat, lax.rem(lon + n_lon - 1, n_lon))
    east = (lat, lax.rem(lon + 1, n_lon))
    barrier = pltpu.get_barrier_semaphore()
    for where in (west, east, north, south):
        pl.semaphore_signal(barrier, inc=1, device_id=where, device_id_type=MESH)

    loads = [
        pltpu.make_async_copy(src, dst, load_sem.at[i])
        for i, (src, dst) in enumerate(
            (
                (inb_hbm, inb),
                (tok_hbm, tok),
                (outb_hbm, outb),
                (dgain_hbm, dgain),
                (dbias_hbm, dbias),
                (dw_hbm, dw),
                (uw_hbm, uw),
                (ugain_hbm, ugain),
                (ubias_hbm, ubias),
                (ow_hbm, ow),
            )
        )
    ]
    for load in loads:
        load.start()

    loads[0].wait()
    start_in = inb[lat]
    count_in = inb[lat + 1] - start_in
    end_all = inb[n_lat]
    start_m = start_in >> 1
    par = start_in & 1
    last_row = jnp.clip(count_in - 1, 0, ROWS - 1)

    def send(k, src, dst, where):
        return pltpu.make_async_remote_copy(
            src_ref=src,
            dst_ref=dst,
            send_sem=send_sem.at[k],
            recv_sem=recv_sem.at[k],
            device_id=where,
            device_id_type=MESH,
        )

    edge_east = send(0, sc.at[3], ew, east)
    main_east = send(1, xa.at[0, 64 : 64 + SEND], xb.at[0, 0:SEND], east)
    edge_west = send(2, sc.at[0], ee, west)
    main_west = send(3, xb.at[1, 0:SEND], xa.at[1, 64 : 64 + SEND], west)
    rows_north = send(4, sc, ls, north)
    rows_south = send(5, sc, ln, south)
    fwd_w_north = send(6, ew, cws, north)
    fwd_w_south = send(7, ew, cwn, south)
    fwd_e_north = send(8, ee, ces, north)
    fwd_e_south = send(9, ee, cen, south)

    zero8 = jnp.zeros((8, LEV * C), BF)

    def stage_edge(x):
        first = tok[:, 0:3, x, :].reshape(12, LEV * C)
        last = [tok[e, last_row][x : x + 1, :] for e in range(E)]
        sc[x] = jnp.concatenate([first] + last, axis=0)

    def stage_main(x, ref, c, at):
        ref[c, at : at + 56, :] = tok[:, :, x, :].reshape(56, LEV * C)
        ref[c, at + 56 : at + 64, :] = zero8

    loads[1].wait()
    stage_edge(3)
    stage_edge(0)
    stage_main(3, xa, 0, 64)
    stage_main(0, xb, 1, 0)
    pl.semaphore_wait(barrier, 4)
    edge_east.start()
    edge_west.start()
    main_east.start()
    main_west.start()
    stage_edge(1)
    stage_edge(2)
    rows_north.start()
    rows_south.start()
    stage_main(1, xa, 0, 0)
    stage_main(2, xa, 1, 0)
    xb[0, 56:64, :] = zero8
    xa[1, 120:128, :] = zero8

    for load in loads[2:]:
        load.wait()
    start_out = outb[lat]
    count_out = outb[lat + 1] - start_out
    skip_m = start_out - start_m
    for q in range(4):
        block = dw[q * C : (q + 1) * C, :]
        zero = jnp.zeros((64, 2 * C), BF)
        we[q * 256 : q * 256 + C, :] = block
        we[q * 256 + C : (q + 1) * 256, :] = zero
        wo[q * 256 : q * 256 + 64, :] = zero
        wo[q * 256 + 64 : (q + 1) * 256, :] = block
    zero64 = jnp.zeros((2 * C, 64), BF)
    for c in range(2):
        for a in range(2):
            q = c * 2 + a
            block = uw[:, q * C : (q + 1) * C]
            at = a * 128
            ua[c, :, at : at + 128] = block[:, 0:128]
            ub[c, 0 : 2 * C, at : at + 128] = jnp.concatenate([block[:, 128:192], zero64], axis=1)
            ub[c, 2 * C : 4 * C, at : at + 128] = jnp.concatenate([zero64, block[:, 0:64]], axis=1)
            uc[c, :, at : at + 128] = block[:, 64:192]
    zero_c = jnp.zeros((C, C), BF)
    small = ow[...]
    bd[0:C, :] = jnp.concatenate([small, zero_c], axis=1)
    bd[C : 2 * C, :] = jnp.concatenate([zero_c, small], axis=1)

    def row_pick(count, a, j, m, e):
        off = 2 * m + a - par
        own = j * 64 + e * 14 + off
        below = count * 64 + j * 16 + e * 3 + (off - count_in)
        above = count * 64 + j * 16 + 12 + e
        is_own = (off >= 0) & (off < count_in)
        is_below = (off >= count_in) & (off < count_in + 3) & (start_in + off < end_all)
        target = jnp.where(is_own, own, jnp.where(is_below, below, jnp.where(off < 0, above, -1)))
        return one_hot(jnp.where(m < MS, target, -1), count * 80)

    row = iota((AR, 1), 0)
    j = (row >= 36).astype(jnp.int32)
    rest = row - 36 * j
    picks_a = [row_pick(2, a, j, rest >> 2, rest & 3) for a in range(2)]
    row = iota((BR, 1), 0)
    picks_b = [row_pick(1, a, 0, row >> 2, row & 3) for a in range(2)]

    gains = []
    for q in range(4):
        one_g = dgain[...].reshape(1, 4 * C)[:, q * C : (q + 1) * C]
        one_b = dbias[...].reshape(1, 4 * C)[:, q * C : (q + 1) * C]
        gains.append((jnp.concatenate([one_g, one_g], axis=1), jnp.concatenate([one_b, one_b], axis=1)))
    one_g = ugain[...].reshape(1, C)
    one_b = ubias[...].reshape(1, C)
    gain2 = jnp.concatenate([one_g, one_g], axis=1)
    bias2 = jnp.concatenate([one_b, one_b], axis=1)

    tile_row = iota((16, LEV * C), 0)

    def halo(below, above):
        return jnp.where(tile_row < 12, below.astype(F32), above.astype(F32)).astype(BF)

    edge_west.wait_recv()
    fwd_e_north.start()
    fwd_e_south.start()
    edge_east.wait_recv()
    fwd_w_north.start()
    fwd_w_south.start()
    rows_north.wait_recv()
    rows_south.wait_recv()
    fwd_e_north.wait_recv()
    fwd_e_south.wait_recv()
    xa[0, 128:144, :] = halo(ls[1], ln[1])
    xa[0, 144:160, :] = halo(ls[3], ln[3])
    xa[1, 128:144, :] = halo(ls[2], ln[2])
    xa[1, 144:160, :] = halo(ces[...], cen[...])
    xb[1, 64:80, :] = halo(ls[0], ln[0])
    main_west.wait_recv()
    for c in range(2):
        for a in range(2):
            ga[c * 2 + a] = dot(picks_a[a], xa[c]).astype(BF)
    norm_rows(ga, AR, nea, noa, AR, gains, AR // 16)
    coa[:, 0:384] = dot(nea[...], we[...]).astype(BF)
    coa[:, 384:768] = dot(noa[...], wo[...]).astype(BF)
    expand(coa[:, 0:384], coa[...], coa[:, 384:768], ua, ub, uc, 0, ya, 0, AR)
    first = jnp.concatenate([coa[lp * AR : lp * AR + BR, :] for lp in range(PAIRS)], axis=0)
    expand(first[:, 0:384], first, first[:, 384:768], ua, ub, uc, 1, ya, 2 * AR, BR)
    row = iota((176, 1), 0)
    x = (row >= 56).astype(jnp.int32) + (row >= 112).astype(jnp.int32)
    rest = row - 56 * x
    e = (rest >= 14).astype(jnp.int32) + (rest >= 28).astype(jnp.int32) + (rest >= 42).astype(jnp.int32)
    o = rest - 14 * e + par
    spot = (o >> 1) * 4 + e
    target = jnp.where(x == 1, 2 * AR + (o & 1) * BR + spot, (o & 1) * AR + spot + (x >> 1) * 36)
    pick = one_hot(jnp.where(row < 168, target, -1), 2 * AR + 2 * BR)
    ea[...] = dot(pick, ya[...]).astype(BF)
    norm_fine(ea, rna, 176, gain2, bias2, 11)
    project(rna, 176, bd, fs, 64, 176)

    fwd_w_north.wait_recv()
    fwd_w_south.wait_recv()
    xb[0, 64:80, :] = halo(cws[...], cwn[...])
    row = iota((64, 1), 0)
    e = (row >= 14).astype(jnp.int32) + (row >= 28).astype(jnp.int32) + (row >= 42).astype(jnp.int32)
    o = row - 14 * e + par
    target = (o & 1) * BR + (o >> 1) * 4 + e
    pick_b = one_hot(jnp.where(row < 56, target, -1), 2 * BR)
    row = iota((224, 1), 0)
    e = (row >= 56).astype(jnp.int32) + (row >= 112).astype(jnp.int32) + (row >= 168).astype(jnp.int32)
    k = (row - 56 * e) >> 2
    x = row & 3
    target = e * 14 + k + jnp.where(x > 0, 8 + x * 56, 0)
    pick_fine = one_hot(jnp.where(k < count_in, target, -1), 240)
    row = iota((64, 1), 0)
    k = (row >> 1) & 7
    target = (k + skip_m) * 4 + (row >> 4)
    live = k < count_out
    pick_m0 = one_hot(jnp.where(live & ((row & 1) == 0), target, -1), BR)
    pick_m1 = one_hot(jnp.where(live & ((row & 1) == 1), target, -1), BR)

    main_east.wait_recv()
    for c in range(2):
        for a in range(2):
            gb[c * 2 + a] = dot(picks_b[a], xb[c]).astype(BF)
    norm_rows(gb, BR, neb, nob, BR, gains, BR // 16)
    cob[:, 0:384] = dot(neb[...], we[...]).astype(BF)
    cob[:, 384:768] = dot(nob[...], wo[...]).astype(BF)
    for lp in range(PAIRS):
        part = dot(pick_m0, cob[lp * BR : (lp + 1) * BR, :]) + dot(pick_m1, coa[lp * AR : lp * AR + BR, :])
        merged[:, :, :, lp * 768 : (lp + 1) * 768] = part.astype(BF).reshape(E, 8, 2, 768)
    expand(cob[:, 0:384], cob[...], cob[:, 384:768], ua, ub, uc, 1, yb, 0, BR)
    eb[...] = dot(pick_b, yb[...]).astype(BF)
    norm_fine(eb, rnb, 64, gain2, bias2, 4)
    project(rnb, 64, bd, fs, 0, 64)
    for lp in range(PAIRS):
        part = dot(pick_fine, fs[:, lp * 384 : (lp + 1) * 384]).astype(BF)
        ups[:, :, :, lp * 384 : (lp + 1) * 384] = part.reshape(E, ROWS, 4, 384)

    edge_east.wait_send()
    main_east.wait_send()
    edge_west.wait_send()
    main_west.wait_send()
    for copy in (rows_north, rows_south, fwd_w_north, fwd_w_south, fwd_e_north, fwd_e_south):
        copy.wait_send()


def copy_out(merged_in, ups_in, merged, ups, sem):
    first = pltpu.make_async_copy(merged_in, merged, sem.at[0])
    second = pltpu.make_async_copy(ups_in, ups, sem.at[1])
    first.start()
    second.start()
    first.wait()
    second.wait()


def solution(mesh):
    n_lat, n_lon = mesh.shape["lat"], mesh.shape["lon"]
    vmem = pl.BlockSpec(memory_space=pltpu.VMEM)
    hbm = pl.BlockSpec(memory_space=pltpu.HBM)
    wide = LEV * C
    outs = (
        jax.ShapeDtypeStruct((E, 8, 2, 2 * wide), BF),
        jax.ShapeDtypeStruct((E, ROWS, 4, wide), BF),
    )

    def body(tok, inb, outb, dgain, dbias, dw, uw, ugain, ubias, ow):
        held = pl.pallas_call(
            functools.partial(kernel, n_lat, n_lon),
            out_shape=outs,
            in_specs=[hbm] * 10,
            out_specs=(vmem, vmem),
            scratch_shapes=[
                pltpu.SMEM((n_lat + 1,), jnp.int32),
                pltpu.SMEM((n_lat + 1,), jnp.int32),
                pltpu.VMEM((4 * C,), F32),
                pltpu.VMEM((4 * C,), F32),
                pltpu.VMEM((C,), F32),
                pltpu.VMEM((C,), F32),
                pltpu.VMEM((E, ROWS, 4, wide), BF),
                pltpu.VMEM((4 * C, 2 * C), BF),
                pltpu.VMEM((2 * C, 4 * C), BF),
                pltpu.VMEM((C, C), BF),
                pltpu.VMEM((2, 160, wide), BF),
                pltpu.VMEM((2, 80, wide), BF),
                pltpu.VMEM((4, 16, wide), BF),
                pltpu.VMEM((16, wide), BF),
                pltpu.VMEM((16, wide), BF),
                pltpu.VMEM((4, 16, wide), BF),
                pltpu.VMEM((4, 16, wide), BF),
                pltpu.VMEM((16, wide), BF),
                pltpu.VMEM((16, wide), BF),
                pltpu.VMEM((16, wide), BF),
                pltpu.VMEM((16, wide), BF),
                pltpu.VMEM((4, AR, wide), BF),
                pltpu.VMEM((4, BR, wide), BF),
                pltpu.VMEM((4 * AR, 1024), BF),
                pltpu.VMEM((4 * AR, 1024), BF),
                pltpu.VMEM((4 * BR, 1024), BF),
                pltpu.VMEM((4 * BR, 1024), BF),
                pltpu.VMEM((1024, 384), BF),
                pltpu.VMEM((1024, 384), BF),
                pltpu.VMEM((2, 384, 256), BF),
                pltpu.VMEM((2, 768, 256), BF),
                pltpu.VMEM((2, 384, 256), BF),
                pltpu.VMEM((384, 384), BF),
                pltpu.VMEM((4 * AR, 768), BF),
                pltpu.VMEM((4 * BR, 768), BF),
                pltpu.VMEM((2 * AR + 2 * BR, wide), BF),
                pltpu.VMEM((2 * BR, wide), BF),
                pltpu.VMEM((176, wide), BF),
                pltpu.VMEM((64, wide), BF),
                pltpu.VMEM((4 * 176, 384), BF),
                pltpu.VMEM((4 * 64, 384), BF),
                pltpu.VMEM((240, wide), BF),
                pltpu.SemaphoreType.DMA((10,)),
                pltpu.SemaphoreType.DMA((10,)),
                pltpu.SemaphoreType.DMA((10,)),
            ],
            compiler_params=pltpu.CompilerParams(
                collective_id=0, has_side_effects=True, vmem_limit_bytes=40000000
            ),
        )(*[pltpu.with_memory_space_constraint(v, pltpu.HBM) for v in (tok, inb, outb, dgain, dbias, dw, uw, ugain, ubias, ow)])
        return pl.pallas_call(
            copy_out,
            out_shape=outs,
            in_specs=[vmem, vmem],
            out_specs=(hbm, hbm),
            scratch_shapes=[pltpu.SemaphoreType.DMA((2,))],
            compiler_params=pltpu.CompilerParams(vmem_limit_bytes=4000000),
        )(*held)

    return jax.shard_map(
        body,
        mesh=mesh,
        in_specs=(P(None, "lat", "lon", None), P(), P(), P(), P(), P(), P(), P(), P(), P()),
        out_specs=(P(None, "lat", "lon", None), P(None, "lat", "lon", None)),
        check_vma=False,
    )
```

time: 44 us -> 37.2 us (0.85)
  the two profiles are of different devices: /device:TPU:1 before, /device:TPU:67 now
where the time goes in v2:
time: 37.2 us; the launch traced here: 37.1 us
  Pallas kernels  36.4 us (98%)
  between operations  0.64 us (2%)
    pallas_call x1, Pallas kernels, body(): pl.pallas_call(functools.partial(kernel, n_lat, n_lon), out_shape=outs, i...  35.4 us
    pallas_call x1, Pallas kernels, body(): pl.pallas_call(copy_out, out_shape=outs, in_specs=[vmem, vmem], out_specs...  1 us

profile of v2, /device:TPU:67, one launch (start us, length us, event | category | flops | bytes accessed | tf_op | source)
XLA Modules:
  0.0 37.1 jit_solution(8987135912727599017)
XLA Ops:
  0.6 35.4 %shard_map.113 = (bf16[4,8,2,3072]{3,2,1,0:T(2,128)(2,1)S(1)}, bf16[4,14,4,1536]{3,2,1,0:T(4,128)(2,1)S(1)}) custom-call(bf16[4,14,4,1536]{3,2,1,0:T(4,128)(2,1)} %tok_hbm.1, s32[17]{0:T(128)} %inb_hbm.1, s32[17]{0:T(128)} %outb_hbm.1, f32[768]{0:T(1024)} %dgain_hbm.1, f32[768]{0:T(1024)} %dbias_hbm.1, bf16[768,384]{1,0:T(8,128)(2,1)} %dw_hbm.1, ...), custom_call_target="tpu_custom_call" | custom-call | tf_op jit(solution)/shard_map/pallas_call | solution.py:430
  36.1 1.0 %shard_map.114 = (bf16[4,8,2,3072]{3,2,1,0:T(2,128)(2,1)}, bf16[4,14,4,1536]{3,2,1,0:T(4,128)(2,1)}) custom-call(bf16[4,8,2,3072]{3,2,1,0:T(2,128)(2,1)S(1)} %get-tuple-element.4.merged_in, bf16[4,14,4,1536]{3,2,1,0:T(4,128)(2,1)S(1)} %get-tuple-element.5.ups_in), custom_call_target="tpu_custom_call" | custom-call | tf_op jit(solution)/shard_map/pallas_call | solution.py:486

commit v3 on v2

--- a/solution.py
+++ b/solution.py
@@ -18,6 +18,8 @@
 MS = 9
 AR = 80
 SEND = 56
+CUTS = (0, 16, 32, 48, 56)
+PIECES = len(CUTS) - 1
 BR = 48
 
 
@@ -142,8 +144,6 @@
     xa,
     xb,
     sc,
-    ew,
-    ee,
     ls,
     ln,
     cws,
@@ -171,6 +171,8 @@
     rna,
     rnb,
     fs,
+    relay,
+    ready,
     load_sem,
     send_sem,
     recv_sem,
@@ -181,9 +183,37 @@
     south = (lax.rem(lat + 1, n_lat), lon)
     west = (lat, lax.rem(lon + n_lon - 1, n_lon))
     east = (lat, lax.rem(lon + 1, n_lon))
+    n_west, n_east = (north[0], west[1]), (north[0], east[1])
+    s_west, s_east = (south[0], west[1]), (south[0], east[1])
     barrier = pltpu.get_barrier_semaphore()
-    for where in (west, east, north, south):
+    has_n = lat > 0
+    has_s = lat < n_lat - 1
+    y = lax.rem(lon, 8)
+    relays = n_lon % 8 == 0 and n_lon > 8 and n_lat % 4 == 0
+    odd = lax.rem(lat // 2, 2) == 1
+    role_7 = odd & (y == 7)
+    role_0 = odd & (y == 0)
+    far_up = (lat, lax.rem(lon + 8, n_lon))
+    far_down = (lat, lax.rem(lon + n_lon - 8, n_lon))
+    pair_up = (lat, lax.rem(lon + 7, n_lon))
+    pair_down = (lat, lax.rem(lon + n_lon - 7, n_lon))
+
+    def tell(where):
         pl.semaphore_signal(barrier, inc=1, device_id=where, device_id_type=MESH)
+
+    def both(first, second):
+        def run():
+            first()
+            second()
+
+        return run
+
+    tell(west)
+    pl.when(has_n)(both(lambda: tell(north), lambda: tell(n_west)))
+    pl.when(has_s)(both(lambda: tell(south), lambda: tell(s_west)))
+    if relays:
+        pl.when(role_7)(both(lambda: tell(far_down), lambda: tell(pair_down)))
+        pl.when(role_0)(both(lambda: tell(far_up), lambda: tell(pair_up)))
 
     loads = [
         pltpu.make_async_copy(src, dst, load_sem.at[i])
@@ -223,18 +253,38 @@
             device_id_type=MESH,
         )
 
-    edge_east = send(0, sc.at[3], ew, east)
     main_east = send(1, xa.at[0, 64 : 64 + SEND], xb.at[0, 0:SEND], east)
-    edge_west = send(2, sc.at[0], ee, west)
     main_west = send(3, xb.at[1, 0:SEND], xa.at[1, 64 : 64 + SEND], west)
     rows_north = send(4, sc, ls, north)
-    rows_south = send(5, sc, ln, south)
-    fwd_w_north = send(6, ew, cws, north)
-    fwd_w_south = send(7, ew, cwn, south)
-    fwd_e_north = send(8, ee, ces, north)
-    fwd_e_south = send(9, ee, cen, south)
+    rows_south = send(5, sc.at[:, 8:16], ln.at[:, 8:16], south)
+    to_ne = send(6, sc.at[3], cws, n_east)
+    to_se = send(7, sc.at[3, 8:16], cwn.at[8:16], s_east)
+    to_nw = send(8, sc.at[0], ces, n_west)
+    to_sw = send(9, sc.at[0, 8:16], cen.at[8:16], s_west)
+
+    up_7, up_0, on_7, on_0 = [], [], [], []
+    for i in range(PIECES):
+        r0, r1 = CUTS[i], CUTS[i + 1]
+        held = relay.at[r0:r1]
+        up_7.append(send(10 + i, xa.at[0, 64 + r0 : 64 + r1], held, far_up))
+        up_0.append(send(10 + i, xb.at[1, r0:r1], held, far_down))
+        on_7.append(send(10 + PIECES + i, held, xb.at[0, r0:r1], pair_down))
+        on_0.append(send(10 + PIECES + i, held, xa.at[1, 64 + r0 : 64 + r1], pair_up))
 
     zero8 = jnp.zeros((8, LEV * C), BF)
+
+    def no_north():
+        ln[...] = jnp.zeros_like(ln)
+        cwn[...] = jnp.zeros_like(cwn)
+        cen[...] = jnp.zeros_like(cen)
+
+    def no_south():
+        ls[...] = jnp.zeros_like(ls)
+        cws[...] = jnp.zeros_like(cws)
+        ces[...] = jnp.zeros_like(ces)
+
+    pl.when(jnp.logical_not(has_n))(no_north)
+    pl.when(jnp.logical_not(has_s))(no_south)
 
     def stage_edge(x):
         first = tok[:, 0:3, x, :].reshape(12, LEV * C)
@@ -245,20 +295,41 @@
         ref[c, at : at + 56, :] = tok[:, :, x, :].reshape(56, LEV * C)
         ref[c, at + 56 : at + 64, :] = zero8
 
+    arrivals = 1 + 2 * has_n.astype(jnp.int32) + 2 * has_s.astype(jnp.int32)
+    if relays:
+        arrivals = arrivals + 2 * (role_7 | role_0).astype(jnp.int32)
+    pl.semaphore_wait(barrier, arrivals)
+
+    def tell_ready(where):
+        pl.semaphore_signal(ready, inc=1, device_id=where, device_id_type=MESH)
+
+    tell_ready(east)
+    pl.when(has_n)(lambda: tell_ready(n_east))
+    pl.when(has_s)(lambda: tell_ready(s_east))
     loads[1].wait()
-    stage_edge(3)
-    stage_edge(0)
+    for x in (3, 0, 1, 2):
+        stage_edge(x)
     stage_main(3, xa, 0, 64)
     stage_main(0, xb, 1, 0)
-    pl.semaphore_wait(barrier, 4)
-    edge_east.start()
-    edge_west.start()
-    main_east.start()
-    main_west.start()
-    stage_edge(1)
-    stage_edge(2)
-    rows_north.start()
-    rows_south.start()
+    pl.when(has_n)(rows_north.start)
+    pl.when(has_s)(rows_south.start)
+    pl.when(has_n)(to_ne.start)
+    pl.when(has_s)(to_se.start)
+    if relays:
+        pl.when(jnp.logical_not(role_7))(main_east.start)
+        for i in range(PIECES):
+            pl.when(role_7)(up_7[i].start)
+    else:
+        main_east.start()
+    pl.semaphore_wait(ready, 1 + has_n.astype(jnp.int32) + has_s.astype(jnp.int32))
+    pl.when(has_n)(to_nw.start)
+    pl.when(has_s)(to_sw.start)
+    if relays:
+        pl.when(jnp.logical_not(role_0))(main_west.start)
+        for i in range(PIECES):
+            pl.when(role_0)(up_0[i].start)
+    else:
+        main_west.start()
     stage_main(1, xa, 0, 0)
     stage_main(2, xa, 1, 0)
     xb[0, 56:64, :] = zero8
@@ -323,22 +394,23 @@
     def halo(below, above):
         return jnp.where(tile_row < 12, below.astype(F32), above.astype(F32)).astype(BF)
 
-    edge_west.wait_recv()
-    fwd_e_north.start()
-    fwd_e_south.start()
-    edge_east.wait_recv()
-    fwd_w_north.start()
-    fwd_w_south.start()
-    rows_north.wait_recv()
-    rows_south.wait_recv()
-    fwd_e_north.wait_recv()
-    fwd_e_south.wait_recv()
+    if relays:
+        for i in range(PIECES):
+            pl.when(role_7)(both(up_7[i].wait_recv, on_7[i].start))
+            pl.when(role_0)(both(up_0[i].wait_recv, on_0[i].start))
+    pl.when(has_s)(both(rows_north.wait_recv, to_nw.wait_recv))
+    pl.when(has_n)(both(rows_south.wait_recv, to_sw.wait_recv))
     xa[0, 128:144, :] = halo(ls[1], ln[1])
     xa[0, 144:160, :] = halo(ls[3], ln[3])
     xa[1, 128:144, :] = halo(ls[2], ln[2])
     xa[1, 144:160, :] = halo(ces[...], cen[...])
     xb[1, 64:80, :] = halo(ls[0], ln[0])
-    main_west.wait_recv()
+    if relays:
+        pl.when(jnp.logical_not(role_7))(main_west.wait_recv)
+        for i in range(PIECES):
+            pl.when(role_7)(on_0[i].wait_recv)
+    else:
+        main_west.wait_recv()
     for c in range(2):
         for a in range(2):
             ga[c * 2 + a] = dot(picks_a[a], xa[c]).astype(BF)
@@ -360,8 +432,8 @@
     norm_fine(ea, rna, 176, gain2, bias2, 11)
     project(rna, 176, bd, fs, 64, 176)
 
-    fwd_w_north.wait_recv()
-    fwd_w_south.wait_recv()
+    pl.when(has_s)(to_ne.wait_recv)
+    pl.when(has_n)(to_se.wait_recv)
     xb[0, 64:80, :] = halo(cws[...], cwn[...])
     row = iota((64, 1), 0)
     e = (row >= 14).astype(jnp.int32) + (row >= 28).astype(jnp.int32) + (row >= 42).astype(jnp.int32)
@@ -381,7 +453,12 @@
     pick_m0 = one_hot(jnp.where(live & ((row & 1) == 0), target, -1), BR)
     pick_m1 = one_hot(jnp.where(live & ((row & 1) == 1), target, -1), BR)
 
-    main_east.wait_recv()
+    if relays:
+        pl.when(jnp.logical_not(role_0))(main_east.wait_recv)
+        for i in range(PIECES):
+            pl.when(role_0)(on_7[i].wait_recv)
+    else:
+        main_east.wait_recv()
     for c in range(2):
         for a in range(2):
             gb[c * 2 + a] = dot(picks_b[a], xb[c]).astype(BF)
@@ -399,12 +476,19 @@
         part = dot(pick_fine, fs[:, lp * 384 : (lp + 1) * 384]).astype(BF)
         ups[:, :, :, lp * 384 : (lp + 1) * 384] = part.reshape(E, ROWS, 4, 384)
 
-    edge_east.wait_send()
-    main_east.wait_send()
-    edge_west.wait_send()
-    main_west.wait_send()
-    for copy in (rows_north, rows_south, fwd_w_north, fwd_w_south, fwd_e_north, fwd_e_south):
-        copy.wait_send()
+    if relays:
+        pl.when(jnp.logical_not(role_7))(main_east.wait_send)
+        pl.when(jnp.logical_not(role_0))(main_west.wait_send)
+        for i in range(PIECES):
+            pl.when(role_7)(both(up_7[i].wait_send, on_7[i].wait_send))
+            pl.when(role_0)(both(up_0[i].wait_send, on_0[i].wait_send))
+    else:
+        main_east.wait_send()
+        main_west.wait_send()
+    for copy in (rows_north, to_ne, to_nw):
+        pl.when(has_n)(copy.wait_send)
+    for copy in (rows_south, to_se, to_sw):
+        pl.when(has_s)(copy.wait_send)
 
 
 def copy_out(merged_in, ups_in, merged, ups, sem):
@@ -446,8 +530,6 @@
                 pltpu.VMEM((2, 160, wide), BF),
                 pltpu.VMEM((2, 80, wide), BF),
                 pltpu.VMEM((4, 16, wide), BF),
-                pltpu.VMEM((16, wide), BF),
-                pltpu.VMEM((16, wide), BF),
                 pltpu.VMEM((4, 16, wide), BF),
                 pltpu.VMEM((4, 16, wide), BF),
                 pltpu.VMEM((16, wide), BF),
@@ -475,9 +557,11 @@
                 pltpu.VMEM((4 * 176, 384), BF),
                 pltpu.VMEM((4 * 64, 384), BF),
                 pltpu.VMEM((240, wide), BF),
+                pltpu.VMEM((56, wide), BF),
+                pltpu.SemaphoreType.REGULAR,
                 pltpu.SemaphoreType.DMA((10,)),
-                pltpu.SemaphoreType.DMA((10,)),
-                pltpu.SemaphoreType.DMA((10,)),
+                pltpu.SemaphoreType.DMA((10 + 2 * PIECES,)),
+                pltpu.SemaphoreType.DMA((10 + 2 * PIECES,)),
             ],
             compiler_params=pltpu.CompilerParams(
                 collective_id=0, has_side_effects=True, vmem_limit_bytes=40000000

time: 37.2 us -> 32.2 us (0.87)
  the two profiles are of different devices: /device:TPU:67 before, /device:TPU:188 now
where the time goes in v3:
time: 32.2 us; the launch traced here: 32 us
  Pallas kernels  31.4 us (98%)
  between operations  0.64 us (2%)
    pallas_call x1, Pallas kernels, body(): pl.pallas_call(functools.partial(kernel, n_lat, n_lon), out_shape=outs, i...  30.4 us
    pallas_call x1, Pallas kernels, body(): pl.pallas_call(copy_out, out_shape=outs, in_specs=[vmem, vmem], out_specs...  1 us

profile of v3, /device:TPU:188, one launch (start us, length us, event | category | flops | bytes accessed | tf_op | source)
XLA Modules:
  0.0 32.0 jit_solution(58105129086808146)
XLA Ops:
  0.6 30.4 %shard_map.113 = (bf16[4,8,2,3072]{3,2,1,0:T(2,128)(2,1)S(1)}, bf16[4,14,4,1536]{3,2,1,0:T(4,128)(2,1)S(1)}) custom-call(bf16[4,14,4,1536]{3,2,1,0:T(4,128)(2,1)} %tok_hbm.1, s32[17]{0:T(128)} %inb_hbm.1, s32[17]{0:T(128)} %outb_hbm.1, f32[768]{0:T(1024)} %dgain_hbm.1, f32[768]{0:T(1024)} %dbias_hbm.1, bf16[768,384]{1,0:T(8,128)(2,1)} %dw_hbm.1, ...), custom_call_target="tpu_custom_call" | custom-call | tf_op jit(solution)/shard_map/pallas_call | solution.py:514
  31.0 1.0 %shard_map.114 = (bf16[4,8,2,3072]{3,2,1,0:T(2,128)(2,1)}, bf16[4,14,4,1536]{3,2,1,0:T(4,128)(2,1)}) custom-call(bf16[4,8,2,3072]{3,2,1,0:T(2,128)(2,1)S(1)} %get-tuple-element.4.merged_in, bf16[4,14,4,1536]{3,2,1,0:T(4,128)(2,1)S(1)} %get-tuple-element.5.ups_in), custom_call_target="tpu_custom_call" | custom-call | tf_op jit(solution)/shard_map/pallas_call | solution.py:570
